TPU v7x, 32 devices: a whole 2x2x4 slice. The times are simulated.
32 devices in a mesh: kx: 2 (over x), ky: 4 (over y, core), kz: 4 (over z).
Axes of the slice: x: 2, y: 2, z: 4, core: 2. Of those that a mesh axis runs over, the one named last changes fastest.
Arguments:
- coefficients: bfloat16 [2, 2, 4, 4, 512, 2048], P(None, 'kx', 'ky', 'kz'), may hold values from -1 to 1
- shift_blocks: int32 [3], replicated, may hold values from 1 to 15, as said below
Outputs:
- centre: float32 [3, 512], replicated
- spread: float32 [3, 512], replicated
- coherence: float32 [3, 2, 4, 4], P(None, 'kx', 'ky', 'kz')
Inputs may be any that keep to these rules, and one draw needn't show every extreme that they name: The coefficients one period further along direction d are those of the first k-point of the string with plane-wave index g read at (g + 128 * shift_blocks[d]) mod 2048.
All inputs are finite; a program needn't handle non-finite values.
Results may differ from a plain program's by a relative error of at most 0.0003.
Values may be sent and summed in bfloat16 or wider, within the bound.
A program may use at most 128 MiB of HBM per device.

v0:
```python
import jax
import jax.numpy as jnp
from jax import lax
from jax.sharding import PartitionSpec as P


def passed_along(value, axis, steps):
    count = lax.axis_size(axis)
    pairs = [(source, (source + steps) % count) for source in range(count)]
    return lax.ppermute(value, axis, pairs)


def pair_measure(own_point, partner):
    bands = own_point.shape[1]
    left_side = jnp.concatenate([own_point[0], own_point[1]], axis=1)
    right_side = jnp.concatenate(
        [
            jnp.concatenate([partner[0], partner[1]], axis=1),
            jnp.concatenate([partner[1], -partner[0]], axis=1),
        ],
        axis=0,
    )
    product = lax.dot_general(
        left_side, right_side, (((1,), (1,)), ((), ())), preferred_element_type=jnp.float32
    )
    real_part = product[:, :bands]
    imag_part = product[:, bands:]
    phases = jnp.arctan2(jnp.diagonal(imag_part), jnp.diagonal(real_part))
    coherence = jnp.sum(real_part * real_part + imag_part * imag_part) / bands
    return (phases, coherence)


def shards(coefficients, shift_blocks):
    planes = coefficients.shape[1]
    bands = coefficients.shape[4]
    width = coefficients.shape[5]
    own_planes = coefficients.reshape(2, planes, bands, width)
    shifts = shift_blocks * 128
    measure = jax.vmap(pair_measure, in_axes=(1, 1))
    next_first = passed_along(own_planes[:, 0], "kx", -1)
    x_wrap = lax.axis_index("kx") == lax.axis_size("kx") - 1
    next_first = jnp.where(x_wrap, jnp.roll(next_first, -shifts[0], axis=-1), next_first)
    x_partner = jnp.concatenate([own_planes[:, 1:], next_first[:, None]], axis=1)
    x_phases, x_coherence = measure(own_planes, x_partner)
    later = passed_along(own_planes, "ky", -1)
    y_wrap = lax.axis_index("ky") == lax.axis_size("ky") - 1
    y_partner = jnp.where(y_wrap, jnp.roll(later, -shifts[1], axis=-1), later)
    y_phases, y_coherence = measure(own_planes, y_partner)
    z_later = passed_along(own_planes, "kz", -1)
    z_wrap = lax.axis_index("kz") == lax.axis_size("kz") - 1
    z_partner = jnp.where(z_wrap, jnp.roll(z_later, -shifts[2], axis=-1), z_later)
    z_phases, z_coherence = measure(own_planes, z_partner)
    phases = jnp.stack([x_phases, y_phases, z_phases])
    coherence = jnp.stack([x_coherence, y_coherence, z_coherence]).reshape(3, planes, 1, 1)
    k_total = planes * lax.axis_size("kx") * lax.axis_size("ky") * lax.axis_size("kz")
    counts = jnp.array(
        [planes * lax.axis_size("kx"), lax.axis_size("ky"), lax.axis_size("kz")], jnp.float32
    )
    phase_sum = jnp.sum(phases, axis=1)
    totals, squares = lax.psum((phase_sum, jnp.sum(phases * phases, axis=1)), ("kx", "ky", "kz"))
    mean_phase = totals / k_total
    variance = squares / k_total - mean_phase * mean_phase
    centre = -counts[:, None] * mean_phase / (2.0 * jnp.pi)
    spread = (counts[:, None] / (2.0 * jnp.pi)) ** 2 * variance
    return (centre, spread, coherence)


def solution(mesh):
    in_specs = (P(None, "kx", "ky", "kz", None, None), P())
    out_specs = (P(), P(), P(None, "kx", "ky", "kz"))
    return jax.shard_map(shards, mesh=mesh, in_specs=in_specs, out_specs=out_specs, check_vma=False)
```

profile of v0, /device:TPU:0, one launch (start us, length us, event | category | flops | bytes accessed | tf_op | source)
XLA Modules:
  0.0 244.8 jit_solution(3515584299984125351)
XLA Ops:
  0.6 5.1 %collective-permute-start.2 = (bf16[2,1,512,2048]{3,2,0,1:T(8,128)(2,1)}, bf16[2,1,512,2048]{3,2,0,1:T(8,128)(2,1)}, u32[]{:S(2)}, u32[]{:S(2)}) collective-permute-start(bf16[2,1,512,2048]{3,2,0,1:T(8,128)(2,1)} %bitcast.83), channel_id=1, source_target_pairs={{0,3},{1,0},{2,1},{3,2},{4,7},{5,4},{6,5},{7,6},{8,11},{9,8},{10,9... | collective-permute-start | bytes 12582920 | tf_op jit(solution)/shard_map/ppermute | solution.py:10
  5.8 0.7 collective-permute-start.1
  6.4 1.5 collective-permute-start
  7.9 0.7 broadcast_multiply_fusion
  11.9 4.8 %slice_bitcast_fusion.5 = (bf16[1,512,2048]{2,1,0:T(8,128)(2,1)}, bf16[1,512,2048]{2,1,0:T(8,128)(2,1)}) fusion(bf16[2,1,1,1,512,2048]{5,4,3,2,1,0:T(8,128)(2,1)} %param.5), kind=kLoop, calls=%fused_computation.48 | loop fusion | bytes 8388608 | tf_op jit(solution)/shard_map/vmap()/squeeze;vmap()/transpose | solution.py:15
  16.6 79.3 %collective-permute-done.2 = bf16[2,1,512,2048]{3,2,0,1:T(8,128)(2,1)} collective-permute-done((bf16[2,1,512,2048]{3,2,0,1:T(8,128)(2,1)}, bf16[2,1,512,2048]{3,2,0,1:T(8,128)(2,1)}, u32[]{:S(2)}, u32[]{:S(2)}) %collective-permute-start.2) | collective-permute-done | bytes 4194336 | tf_op jit(solution)/shard_map/ppermute | solution.py:10
  95.9 6.5 %fusion.38 = bf16[2,1,512,2048]{3,2,1,0:T(8,128)(2,1)S(1)} fusion(bf16[2,1,512,2048]{3,2,0,1:T(8,128)(2,1)} %collective-permute-done.2, s32[]{:T(128)S(6)} %select_n.69, pred[]{:T(512)S(6)} %eq.15), kind=kLoop, calls=%fused_computation.77 | loop fusion | flops 10485760 | bytes 8388613 | tf_op jit(solution)/shard_map/jit(_where)/select_n | solution.py:51
  102.4 1.5 fusion.34
  103.8 1.6 slice_bitcast_fusion.1
  105.4 7.6 %fusion.37 = bf16[2,1,512,2048]{3,2,1,0:T(8,128)(2,1)S(1)} fusion(bf16[2,1,512,2048]{3,2,0,1:T(8,128)(2,1)} %collective-permute-done.1, s32[]{:T(128)S(6)} %select_n.67, pred[]{:T(512)S(6)} %eq.14), kind=kLoop, calls=%fused_computation.76 | loop fusion | flops 10485760 | bytes 8388613 | tf_op jit(solution)/shard_map/jit(_where)/select_n | solution.py:47
  113.0 1.5 fusion.33
  114.5 1.5 slice_bitcast_fusion.3
  116.0 6.6 %fusion.26 = bf16[2,512,2048]{2,1,0:T(8,128)(2,1)S(1)} fusion(bf16[2,512,2048]{2,1,0:T(8,128)(2,1)} %collective-permute-done, s32[]{:T(128)S(6)} %select_n.58, pred[]{:T(512)S(6)} %eq.13), kind=kLoop, calls=%fused_computation.41 | loop fusion | flops 10485760 | bytes 8388613 | tf_op jit(solution)/shard_map/jit(_where)/select_n | solution.py:42
  123.0 8.1 %fusion.29 = f32[1,512,1024]{2,1,0:T(8,128)} fusion(bf16[1,512,2048]{2,1,0:T(8,128)(2,1)S(1)} %get-tuple-element.7, bf16[1,512,2048]{2,1,0:T(8,128)(2,1)S(1)} %get-tuple-element.8, bf16[1,512,2048]{2,1,0:T(8,128)(2,1)S(1)} %get-tuple-element.6, bf16[1,512,2048]{2,1,0:T(8,128)(2,1)} %get-tuple-element.10, bf16[1,512,2048]{2,1,0:T(8,128)(2,1)} %get-tuple-element.9), kind=kOutput, calls=%fused_computation.51 | convolution fusion | flops 4336910336 | bytes 12582912 | tf_op jit(solution)/shard_map/vmap()/dot_general | solution.py:23
  131.1 2.5 %add_reduce_fusion.2 = (f32[]{:T(128)}, f32[512,512]{1,0:T(8,128)S(1)}, f32[512,512]{1,0:T(8,128)S(1)}) fusion(f32[1,512,1024]{2,1,0:T(8,128)} %fusion.29), kind=kLoop, calls=%fused_computation.54 | loop fusion | flops 1048575 | bytes 4194308 | tf_op jit(solution)/shard_map/vmap()/reduce_sum | solution.py:29
  133.6 4.5 %gather_fusion.1 = f32[512]{0:T(512)S(1)} fusion(f32[512,512]{1,0:T(8,128)S(1)} %get-tuple-element.12, s32[512]{0:T(512)S(1)} %bitcast.77), kind=kCustom, calls=%fused_computation.1 | custom fusion | bytes 8192 | tf_op jit(solution)/shard_map/vmap(jit(diagonal))/cond/branch_0_fun/gather | solution.py:28
  138.1 4.5 %gather_fusion = f32[512]{0:T(512)S(1)} fusion(f32[512,512]{1,0:T(8,128)S(1)} %get-tuple-element.13, s32[512]{0:T(512)S(1)} %bitcast.78), kind=kCustom, calls=%fused_computation | custom fusion | bytes 8192 | tf_op jit(solution)/shard_map/vmap(jit(diagonal))/cond/branch_0_fun/gather | solution.py:28
  142.7 6.5 %fusion.22 = bf16[2,1,512,2048]{3,2,0,1:T(8,128)(2,1)S(1)} fusion(bf16[2,1,512,2048]{3,2,0,1:T(8,128)(2,1)} %collective-permute-done.2, s32[]{:T(128)S(6)} %select_n.69, pred[]{:T(512)S(6)} %eq.15), kind=kLoop, calls=%fused_computation.37 | loop fusion | flops 10485760 | bytes 8388613 | tf_op jit(solution)/shard_map/jit(_where)/select_n | solution.py:51
  149.3 1.4 copy-done.2
  150.8 0.6 copy-done.3
  151.4 8.1 %fusion.27 = f32[1,512,1024]{2,1,0:T(8,128)} fusion(bf16[1,512,2048]{2,1,0:T(8,128)(2,1)S(1)} %copy-done.2, bf16[1,512,2048]{2,1,0:T(8,128)(2,1)S(1)} %slice_bitcast_fusion, bf16[1,512,2048]{2,1,0:T(8,128)(2,1)S(1)} %copy-done.3, bf16[1,512,2048]{2,1,0:T(8,128)(2,1)} %get-tuple-element.10, bf16[1,512,2048]{2,1,0:T(8,128)(2,1)} %get-tuple-element.9), kind=kOutput, calls=%fused_computation.49 | convolution fusion | flops 4336910336 | bytes 12582912 | tf_op jit(solution)/shard_map/vmap()/dot_general | solution.py:23
  159.5 2.5 %add_reduce_fusion = (f32[]{:T(128)}, f32[512,512]{1,0:T(8,128)S(1)}, f32[512,512]{1,0:T(8,128)S(1)}) fusion(f32[1,512,1024]{2,1,0:T(8,128)} %fusion.27), kind=kLoop, calls=%fused_computation.52 | loop fusion | flops 1048575 | bytes 4194308 | tf_op jit(solution)/shard_map/vmap()/reduce_sum | solution.py:29
  163.3 4.5 %gather_fusion.5 = f32[512]{0:T(512)S(1)} fusion(f32[512,512]{1,0:T(8,128)S(1)} %get-tuple-element.18, s32[512]{0:T(512)S(1)} %bitcast.79), kind=kCustom, calls=%fused_computation.5 | custom fusion | bytes 8192 | tf_op jit(solution)/shard_map/vmap(jit(diagonal))/cond/branch_0_fun/gather | solution.py:28
  167.8 4.5 %gather_fusion.4 = f32[512]{0:T(512)S(1)} fusion(f32[512,512]{1,0:T(8,128)S(1)} %get-tuple-element.19, s32[512]{0:T(512)S(1)} %bitcast.80), kind=kCustom, calls=%fused_computation.4 | custom fusion | bytes 8192 | tf_op jit(solution)/shard_map/vmap(jit(diagonal))/cond/branch_0_fun/gather | solution.py:28
  172.3 7.8 %fusion.24 = bf16[2,1,512,2048]{3,2,0,1:T(8,128)(2,1)S(1)} fusion(bf16[2,1,512,2048]{3,2,0,1:T(8,128)(2,1)} %collective-permute-done.1, s32[]{:T(128)S(6)} %select_n.67, pred[]{:T(512)S(6)} %eq.14), kind=kLoop, calls=%fused_computation.39 | loop fusion | flops 10485760 | bytes 8388613 | tf_op jit(solution)/shard_map/jit(_where)/select_n | solution.py:47
  180.3 1.4 copy-done
  182.3 8.1 %fusion.28 = f32[1,512,1024]{2,1,0:T(8,128)} fusion(bf16[1,512,2048]{2,1,0:T(8,128)(2,1)S(1)} %copy-done, bf16[1,512,2048]{2,1,0:T(8,128)(2,1)S(1)} %slice_bitcast_fusion.2, bf16[1,512,2048]{2,1,0:T(8,128)(2,1)S(1)} %copy-done.1, bf16[1,512,2048]{2,1,0:T(8,128)(2,1)} %get-tuple-element.10, bf16[1,512,2048]{2,1,0:T(8,128)(2,1)} %get-tuple-element.9), kind=kOutput, calls=%fused_computation.50 | convolution fusion | flops 4336910336 | bytes 12582912 | tf_op jit(solution)/shard_map/vmap()/dot_general | solution.py:23
  190.4 2.5 %add_reduce_fusion.1 = (f32[]{:T(128)}, f32[512,512]{1,0:T(8,128)S(1)}, f32[512,512]{1,0:T(8,128)S(1)}) fusion(f32[1,512,1024]{2,1,0:T(8,128)} %fusion.28), kind=kLoop, calls=%fused_computation.53 | loop fusion | flops 1048575 | bytes 4194308 | tf_op jit(solution)/shard_map/vmap()/reduce_sum | solution.py:29
  193.6 4.5 %gather_fusion.3 = f32[512]{0:T(512)S(1)} fusion(f32[512,512]{1,0:T(8,128)S(1)} %get-tuple-element.15, s32[512]{0:T(512)S(1)} %bitcast.81), kind=kCustom, calls=%fused_computation.3 | custom fusion | bytes 8192 | tf_op jit(solution)/shard_map/vmap(jit(diagonal))/cond/branch_0_fun/gather | solution.py:28
  198.1 4.5 %gather_fusion.2 = f32[512]{0:T(512)S(1)} fusion(f32[512,512]{1,0:T(8,128)S(1)} %get-tuple-element.16, s32[512]{0:T(512)S(1)} %bitcast.82), kind=kCustom, calls=%fused_computation.2 | custom fusion | bytes 8192 | tf_op jit(solution)/shard_map/vmap(jit(diagonal))/cond/branch_0_fun/gather | solution.py:28
  202.8 40.7 %all-reduce = (f32[3,512]{1,0:T(4,128)S(1)}, f32[3,512]{1,0:T(4,128)S(1)}) all-reduce(f32[3,512]{1,0:T(4,128)S(1)} %maximum_bitcast_fusion.16, f32[3,512]{1,0:T(4,128)S(1)} %maximum_multiply_fusion), channel_id=1, replica_groups=mesh['kx'=2,'ky'=4,'kz'=4] {'kx','ky','kz'}, use_global_device_ids=true, to_apply=%region_0.2 | all-reduce | flops 3072 | bytes 24576 | tf_op jit(solution)/shard_map/psum | solution.py:60
  244.2 0.7 subtract_multiply_fusion
  (22 shorter events, 2.6 us)
Async XLA Ops:
  0.6 95.3 %collective-permute-start.2 = (bf16[2,1,512,2048]{3,2,0,1:T(8,128)(2,1)}, bf16[2,1,512,2048]{3,2,0,1:T(8,128)(2,1)}, u32[]{:S(2)}, u32[]{:S(2)}) collective-permute-start(bf16[2,1,512,2048]{3,2,0,1:T(8,128)(2,1)} %bitcast.83), channel_id=1, source_target_pairs={{0,3},{1,0},{2,1},{3,2},{4,7},{5,4},{6,5},{7,6},{8,11},{9,8},{10,9... | collective-permute-start | bytes 12582920 | tf_op jit(solution)/shard_map/ppermute | solution.py:10
  5.8 99.7 %collective-permute-start.1 = (bf16[2,1,512,2048]{3,2,0,1:T(8,128)(2,1)}, bf16[2,1,512,2048]{3,2,0,1:T(8,128)(2,1)}, u32[]{:S(2)}, u32[]{:S(2)}) collective-permute-start(bf16[2,1,512,2048]{3,2,0,1:T(8,128)(2,1)} %bitcast.84), channel_id=1, source_target_pairs={{0,12},{4,0},{8,4},{12,8},{1,13},{5,1},{9,5},{13,9},{2,14},{6,2},{... | collective-permute-start | bytes 12582920 | tf_op jit(solution)/shard_map/ppermute | solution.py:10
  6.4 109.6 %collective-permute-start = (bf16[2,512,2048]{2,1,0:T(8,128)(2,1)}, bf16[2,512,2048]{2,1,0:T(8,128)(2,1)}, u32[]{:S(2)}, u32[]{:S(2)}) collective-permute-start(bf16[2,512,2048]{2,1,0:T(8,128)(2,1)} %bitcast.85), channel_id=1, source_target_pairs={{0,16},{16,0},{1,17},{17,1},{2,18},{18,2},{3,19},{19,3},{4,20},{20... | collective-permute-start | bytes 12582920 | tf_op jit(solution)/shard_map/ppermute | solution.py:10
  149.2 1.6 copy-start.2
  149.2 2.2 copy-start.3
  180.1 1.6 copy-start
  180.1 2.2 copy-start.1
  190.4 53.7 %copy-start.4 = (f32[3]{0:T(128)S(1)}, f32[3]{0:T(128)}, u32[]{:S(2)}) copy-start(f32[3]{0:T(128)} %constant.98) | copy-start | bytes 40
  190.4 53.7 %copy-start.5 = (f32[3]{0:T(128)S(1)}, f32[3]{0:T(128)}, u32[]{:S(2)}) copy-start(f32[3]{0:T(128)} %constant.95) | copy-start | bytes 40
where the time goes:
time: 245 us
  waiting for transfers between devices  79.3 us (32%)
  other arithmetic  47.6 us (19%)
  blocking collectives  40.7 us (17%)
  local copies, waits for them, and re-layouts  40.1 us (16%)
  matrix products  24.3 us (10%)
  starting transfers between devices  7.3 us (3%)
  between operations  5.43 us (2%)
    ppermute x3, waiting for transfers between devices, passed_along(): return lax.ppermute(value, axis, pairs)  79.3 us
    psum x1, blocking collectives, shards(): lax.psum((phase_sum, jnp.sum(phases * phases, axis=1)), ('kx', 'ky', 'kz'))  40.7 us
    gather x6, local copies, waits for them, and re-layouts, pair_measure(): phases = jnp.arctan2(jnp.diagonal(imag_part), jnp.diagonal(real_part))  27.1 us
    dot_general x3, matrix products, pair_measure(): lax.dot_general(left_side, right_side, (((1,), (1,)), ((), ())), preferre...  24.3 us
    select_n x2, other arithmetic, shards(): y_partner = jnp.where(y_wrap, jnp.roll(later, -shifts[1], axis=-1), later)  15.3 us
    select_n x2, other arithmetic, shards(): jnp.where(z_wrap, jnp.roll(z_later, -shifts[2], axis=-1), z_later)  12.9 us
    reduce_sum x3, other arithmetic, pair_measure(): coherence = jnp.sum(real_part * real_part + imag_part * imag_part) / bands  7.5 us
    ppermute x3, starting transfers between devices, passed_along(): return lax.ppermute(value, axis, pairs)  7.3 us
  transfers between devices with their start and end apart: 3, of which 1 were waited for; matrix products, arithmetic and copies ran while one was open for 11% of the time, Pallas kernels for 0%

commit v1 on v0

v1 whole, which is shorter than its diff:
```python
import functools

import jax
import jax.numpy as jnp
from jax import lax
from jax.experimental import pallas as pl
from jax.experimental.pallas import tpu as pltpu
from jax.sharding import PartitionSpec as P

MESH = pl.DeviceIdType.MESH
AXES = ("kx", "ky", "kz")
LANES = 128
ROWS = 256
STRIP = 32


def greeted(count):
    return range(1, count) if count > 4 else sorted({1, count - 1})


def merged(parts, count):
    mean = functools.reduce(jnp.add, [part[0] for part in parts]) / len(parts)
    square = functools.reduce(jnp.add, [part[1] for part in parts])
    apart = functools.reduce(jnp.add, [(part[0] - mean) * (part[0] - mean) for part in parts])
    return mean, square + count * apart


def kernel(sizes, shift_ref, a_ref, centre_ref, spread_ref, coherence_ref,
           own, partner, rolled, diag_re, diag_im, total, stats, heard,
           own_sem, send_sem, recv_sem, stat_send, stat_recv):
    planes, bands, width = own.shape[1:]
    chunks, cut = partner.shape[1], partner.shape[3]
    tiles, row_tiles = width // LANES, bands // ROWS
    place = [lax.axis_index(axis) for axis in AXES]
    points = [(d, p) for d in range(3) for p in range(planes)]

    def beside(d, step):
        return {AXES[d]: lax.rem(place[d] + step, sizes[d])}

    load = pltpu.make_async_copy(a_ref, own, own_sem)
    load.start()
    barrier = pltpu.get_barrier_semaphore()
    greetings = 0
    for d in range(3):
        for step in greeted(sizes[d]):
            pl.semaphore_signal(barrier, inc=1, device_id=beside(d, step), device_id_type=MESH)
            greetings += 1
    pl.semaphore_wait(barrier, greetings)

    def copy_of(i, c):
        d, p = points[i]
        source = (p + 1) % planes if d == 0 else p
        return pltpu.make_async_remote_copy(
            src_ref=a_ref.at[:, source, pl.ds(pl.multiple_of(c * cut, cut), cut), :],
            dst_ref=partner.at[i, c],
            send_sem=send_sem.at[i, c],
            recv_sem=recv_sem.at[i, c],
            device_id=beside(d, sizes[d] - 1),
            device_id_type=MESH,
        )

    def inner_copy(i, c):
        p = points[i][1]
        return pltpu.make_async_copy(
            a_ref.at[:, p + 1, pl.ds(pl.multiple_of(c * cut, cut), cut), :], partner.at[i, c], recv_sem.at[i, c]
        )

    def inner(i):
        d, p = points[i]
        return d == 0 and p < planes - 1

    def launch(c, carry):
        for i in range(len(points)):
            (inner_copy(i, c) if inner(i) else copy_of(i, c)).start()
        return carry

    lax.fori_loop(0, chunks, launch, 0)

    total[...] = jnp.zeros_like(total)
    diag_re[...] = jnp.zeros_like(diag_re)
    diag_im[...] = jnp.zeros_like(diag_im)
    load.wait()
    for i, (d, p) in enumerate(points):
        wraps = place[d] == sizes[d] - 1
        shift = 0 if inner(i) else jnp.where(wraps, shift_ref[d], 0)

        moves = [] if inner(i) else [(LANES << bit, (shift >> bit) & 1 == 1) for bit in range((tiles - 1).bit_length())]

        def turn(block, carry, i=i, p=p, moves=moves):
            rows = pl.ds(pl.multiple_of(block * STRIP, STRIP), STRIP)
            for part in range(2):
                value = own[part, p, rows, :]
                for amount, taken in moves:
                    moved = jnp.concatenate([value[:, width - amount:], value[:, :width - amount]], axis=1)
                    value = jnp.where(taken, moved, value)
                rolled[i, part, rows, :] = value
            return carry

        lax.fori_loop(0, bands // STRIP, turn, 0)

    row = lax.broadcasted_iota(jnp.int32, (ROWS, cut), 0)
    column = lax.broadcasted_iota(jnp.int32, (ROWS, cut), 1)

    def arrived(i, c):
        (inner_copy(i, c).wait if inner(i) else copy_of(i, c).wait_recv)()

    def measure(i, c, r):
        left = rolled[i, :, pl.ds(pl.multiple_of(r * ROWS, ROWS), ROWS), :].reshape(2 * ROWS, width)
        right = partner[i, c].reshape(2 * cut, width)
        product = lax.dot_general(left, right, (((1,), (1,)), ((), ())), preferred_element_type=jnp.float32)
        re = product[:ROWS, :cut] + product[ROWS:, cut:]
        im = product[:ROWS, cut:] - product[ROWS:, :cut]
        squares = re * re + im * im
        total[i] += jnp.sum(squares.reshape(ROWS // 8, 8, cut), axis=0)
        same = row + r * ROWS == column + c * cut
        diag_re[i, pl.ds(c, 1), :] += jnp.sum(jnp.where(same, re, 0.0), axis=0, keepdims=True)
        diag_im[i, pl.ds(c, 1), :] += jnp.sum(jnp.where(same, im, 0.0), axis=0, keepdims=True)

    def rest(c, first, count):
        def one(r, carry):
            for i in order:
                measure(i, c, r)
            return carry
        lax.fori_loop(first, first + count, one, 0)

    order = [i for d in (1, 0, 2) for i, point in enumerate(points) if point[0] == d]

    def chunk(c, carry):
        for i in order:
            arrived(i, c)
        rest(c, 0, row_tiles)
        return carry

    lax.fori_loop(0, chunks - 1, chunk, 0)
    last = chunks - 1
    for i in order:
        arrived(i, last)
    rest(last, row_tiles - 1, 1)
    phases = jnp.arctan2(diag_im[...], diag_re[...])
    groups = phases.reshape(3, planes, chunks, cut)
    mean, square = merged([(groups[:, p], jnp.zeros_like(groups[:, p])) for p in range(planes)], 1.0)
    count = float(planes)

    def stat_copy(d, step):
        return pltpu.make_async_remote_copy(
            src_ref=stats.at[d],
            dst_ref=heard[d].at[step - 1],
            send_sem=stat_send[d].at[step - 1],
            recv_sem=stat_recv[d].at[step - 1],
            device_id=beside(d, step),
            device_id_type=MESH,
        )

    for d in range(3):
        stats[d, 0] = mean
        stats[d, 1] = square
        for step in range(1, sizes[d]):
            stat_copy(d, step).start()
        if d == 0 and row_tiles > 1:
            rest(last, 0, row_tiles - 1)
            for i in range(len(points)):
                coherence_ref[i:i + 1, :] = jnp.full((1, LANES), 1.0 / bands, jnp.float32) * jnp.sum(total[i])
        for step in range(1, sizes[d]):
            stat_copy(d, step).wait_recv()
        members = [(mean, square)] + [(heard[d][step - 1, 0], heard[d][step - 1, 1]) for step in range(1, sizes[d])]
        ordered = []
        for slot in range(sizes[d]):
            entry = None
            for step in range(sizes[d]):
                owner = lax.rem(place[d] - step + sizes[d], sizes[d])
                if entry is None:
                    entry = members[step]
                else:
                    entry = tuple(jnp.where(owner == slot, new, old) for new, old in zip(members[step], entry))
            ordered.append(entry)
        mean, square = merged(ordered, count)
        count *= sizes[d]

    lengths = (planes * sizes[0], sizes[1], sizes[2])
    for d in range(3):
        scale = lengths[d] / (2.0 * jnp.pi)
        for c in range(chunks):
            lanes = slice(c * cut, (c + 1) * cut)
            centre_ref[d:d + 1, lanes] = -scale * mean[d, c:c + 1, :]
            spread_ref[d:d + 1, lanes] = scale * scale * (square[d, c:c + 1, :] / count)

    for d in range(3):
        for step in range(1, sizes[d]):
            stat_copy(d, step).wait_send()

    def sent(c, carry):
        for i in range(len(points)):
            if not inner(i):
                copy_of(i, c).wait_send()
        return carry

    lax.fori_loop(0, chunks, sent, 0)


def solution(mesh):
    sizes = tuple(mesh.shape[axis] for axis in AXES)

    def shards(coefficients, shift_blocks):
        planes, bands, width = coefficients.shape[1], coefficients.shape[4], coefficients.shape[5]
        own_planes = coefficients.reshape(2, planes, bands, width)
        chunks = bands // LANES
        pairs = 3 * planes
        vmem = pl.BlockSpec(memory_space=pltpu.VMEM)
        centre, spread, coherence = pl.pallas_call(
            functools.partial(kernel, sizes),
            out_shape=(
                jax.ShapeDtypeStruct((3, bands), jnp.float32),
                jax.ShapeDtypeStruct((3, bands), jnp.float32),
                jax.ShapeDtypeStruct((pairs, LANES), jnp.float32),
            ),
            in_specs=[pl.BlockSpec(memory_space=pltpu.SMEM), pl.BlockSpec(memory_space=pl.ANY)],
            out_specs=(vmem, vmem, vmem),
            scratch_shapes=[
                pltpu.VMEM((2, planes, bands, width), jnp.bfloat16),
                pltpu.VMEM((pairs, chunks, 2, LANES, width), jnp.bfloat16),
                pltpu.VMEM((pairs, 2, bands, width), jnp.bfloat16),
                pltpu.VMEM((pairs, chunks, LANES), jnp.float32),
                pltpu.VMEM((pairs, chunks, LANES), jnp.float32),
                pltpu.VMEM((pairs, 8, LANES), jnp.float32),
                pltpu.VMEM((3, 2, 3, chunks, LANES), jnp.float32),
                [pltpu.VMEM((size - 1, 2, 3, chunks, LANES), jnp.float32) for size in sizes],
                pltpu.SemaphoreType.DMA,
                pltpu.SemaphoreType.DMA((pairs, chunks)),
                pltpu.SemaphoreType.DMA((pairs, chunks)),
                [pltpu.SemaphoreType.DMA((size - 1,)) for size in sizes],
                [pltpu.SemaphoreType.DMA((size - 1,)) for size in sizes],
            ],
            compiler_params=pltpu.CompilerParams(
                collective_id=0, has_side_effects=True, vmem_limit_bytes=60 * 1024 * 1024
            ),
        )(shift_blocks, own_planes)
        return centre, spread, coherence[:, :1].reshape(3, planes, 1, 1)

    in_specs = (P(None, "kx", "ky", "kz", None, None), P())
    out_specs = (P(), P(), P(None, "kx", "ky", "kz"))
    return jax.shard_map(shards, mesh=mesh, in_specs=in_specs, out_specs=out_specs, check_vma=False)
```

time: 245 us -> 117 us (0.48)
  Pallas kernels: 0 us -> 112 us
  waiting for transfers between devices: 79.3 us -> 0 us
  other arithmetic: 47.6 us -> 0 us
  blocking collectives: 40.7 us -> 0 us
  local copies, waits for them, and re-layouts: 40.1 us -> 3.87 us
  matrix products: 24.3 us -> 0 us
  starting transfers between devices: 7.3 us -> 0 us
  between operations: 5.43 us -> 0.64 us
    pallas_call x0 -> x1, Pallas kernels: none -> 112 us  [shards(): pl.pallas_call(functools.partial(kernel, sizes), out_shape=(jax.ShapeDtyp...]
    ppermute x3 -> x0, waiting for transfers between devices: 79.3 us -> none  [passed_along(): return lax.ppermute(value, axis, pairs)]
    psum x1 -> x0, blocking collectives: 40.7 us -> none  [shards(): lax.psum((phase_sum, jnp.sum(phases * phases, axis=1)), ('kx', 'ky', 'kz'))]
    select_n x5 -> x0, other arithmetic: 34.8 us -> none  [the longest x2 15.3 us: shards(): y_partner = jnp.where(y_wrap, jnp.roll(later, -shifts[1], axis=-1), later)]
    gather x6 -> x0, local copies, waits for them, and re-layouts: 27.1 us -> none  [pair_measure(): phases = jnp.arctan2(jnp.diagonal(imag_part), jnp.diagonal(real_part))]
    dot_general x3 -> x0, matrix products: 24.3 us -> none  [pair_measure(): lax.dot_general(left_side, right_side, (((1,), (1,)), ((), ())), preferre...]
    transpose x5 -> x0, local copies, waits for them, and re-layouts: 8.18 us -> none  [the longest x1 4.76 us: pair_measure(): left_side = jnp.concatenate([own_point[0], own_point[1]], axis=1)]
    reduce_sum x4 -> x0, other arithmetic: 7.52 us -> none  [the longest x3 7.5 us: pair_measure(): coherence = jnp.sum(real_part * real_part + imag_part * imag_part) / bands]
  transfers between devices with their start and end apart: 3 -> 0, of which waited for: 1 -> 0; matrix products, arithmetic and copies ran while one was open for 11% -> 0% of each run, Pallas kernels for 0% -> 0%
where the time goes in v1:
time: 117 us; the launch traced here: 116 us
  Pallas kernels  112 us (96%)
  local copies, waits for them, and re-layouts  3.87 us (3%)
    pallas_call x1, Pallas kernels, shards(): pl.pallas_call(functools.partial(kernel, sizes), out_shape=(jax.ShapeDtyp...  112 us
    unnamed x2, local copies, waits for them, and re-layouts  2.59 us

profile of v1, /device:TPU:0, one launch (start us, length us, event | category | flops | bytes accessed | tf_op | source)
XLA Modules:
  0.0 116.2 jit_solution(6876023372910401374)
XLA Ops:
  0.6 111.7 %shard_map.49 = (f32[3,512]{1,0:T(4,128)}, f32[3,512]{1,0:T(4,128)}, f32[3,128]{1,0:T(4,128)}) custom-call(s32[3]{0:T(128)} %shift_ref.1, bf16[2,1,512,2048]{3,2,1,0:T(8,128)(2,1)} %bitcast.2), custom_call_target="tpu_custom_call" | custom-call | tf_op jit(solution)/shard_map/pallas_call | solution.py:209
  112.3 1.3 %slice_reduce_fusion = f32[3]{0:T(128)} fusion(f32[3,128]{1,0:T(4,128)} %get-tuple-element.8), kind=kLoop, calls=%fused_computation | loop fusion | bytes 24 | tf_op jit(solution)/shard_map/slice | solution.py:237
  113.6 1.3 %copy.7 = f32[3,512]{1,0:T(4,128)} copy(f32[3,512]{1,0:T(4,128)} %get-tuple-element.12) | data formatting | bytes 12288
  114.9 1.3 %copy.8 = f32[3,512]{1,0:T(4,128)} copy(f32[3,512]{1,0:T(4,128)} %get-tuple-element.13) | data formatting | bytes 12288
